TPU v7x, 32 devices: a whole 2x2x4 slice. The times are simulated.
32 devices in a mesh: cuts: 2 (over x), wide: 8 (over z, y), batch: 2 (over core).
Axes of the slice: x: 2, y: 2, z: 4, core: 2. Of those that a mesh axis runs over, the one named last changes fastest.
Arguments:
- initial: bfloat16 [2, 64, 2, 2, 256, 256], P('batch', 'cuts', None, None, None, 'wide'), parts along dimension 1, may hold values from -6 to 6
- branches: bfloat16 [8, 2, 2, 256, 2, 256], P(None, None, None, 'batch'), may hold values from -0.1875 to 0.1875
- projectors: float32 [8, 2, 2, 2], replicated, may hold values from -4 to 4
- bits: int32 [2, 8], P('batch'), may hold values from 0 to 1
Outputs:
- amplitudes: float32 [2, 64, 2, 2, 256, 256], P('batch', 'cuts', None, None, 'wide'), parts along dimension 1
There are 2 independent parts, one for each index of `cuts`. A program takes and returns all parts, laid end to end along the dimension named above; an argument that names none is the same for every part. Nothing has to cross between parts.
Inputs may be any that keep to these rules, and one draw needn't show every extreme that they name: `bits`: each entry is a bit.
All inputs are finite; a program needn't handle non-finite values.
Results may differ from a plain program's by a relative error of at most 0.014.
Values may be sent and summed in bfloat16 or wider, within the bound.
A program may use at most 64 MiB of HBM per device.

v0:
```python
import jax
import jax.numpy as jnp
from jax import lax
from jax.sharding import PartitionSpec as P


def contract(state, branch, select):
    prod = jnp.einsum("ncphuv,thugw->ncptgvw", state, branch, preferred_element_type=jnp.float32)
    real_part = prod[:, :, 0, 0] - prod[:, :, 1, 1]
    imag_part = prod[:, :, 0, 1] + prod[:, :, 1, 0]
    proj_re = select[:, 0][:, None, :, None, None]
    proj_im = select[:, 1][:, None, :, None, None]
    out_re = proj_re * real_part - proj_im * imag_part
    out_im = proj_re * imag_part + proj_im * real_part
    return jnp.stack([out_re, out_im], axis=2)


def advance(block, branch, select, final):
    result = contract(block, branch, select)
    if final:
        return result
    return result.astype(jnp.bfloat16)


def branch_of(branches, step):
    return lax.all_gather(branches[step], "batch", axis=2, tiled=True)


def select_of(projectors, bits, step):
    chosen = (bits[:, step] == 1)[:, None, None]
    return jnp.where(chosen, projectors[step, 1][None], projectors[step, 0][None])


def shards(initial, branches, projectors, bits):
    steps_total = branches.shape[0]
    state = lax.all_to_all(initial, "wide", split_axis=1, concat_axis=5, tiled=True)
    for step in range(steps_total):
        branch = branch_of(branches, step)
        select = select_of(projectors, bits, step)
        state = advance(state, branch, select, step == steps_total - 1)
    return lax.all_to_all(state, "wide", split_axis=4, concat_axis=1, tiled=True)


def solution(mesh):
    in_specs = (
        P("batch", "cuts", None, None, None, "wide"),
        P(None, None, None, "batch", None, None),
        P(),
        P("batch", None),
    )
    out_specs = P("batch", "cuts", None, None, "wide", None)
    return jax.shard_map(shards, mesh=mesh, in_specs=in_specs, out_specs=out_specs, check_vma=False)
```

profile of v0, /device:TPU:0, one launch (start us, length us, event | category | flops | bytes accessed | tf_op | source)
XLA Modules:
  0.0 227.0 jit_solution(12118872197756063000)
XLA Ops:
  6.5 0.0 all-gather.17.cloned.1.call-start
  6.5 5.4 %fusion.39 = (bf16[1,2,2,128,2,256]{5,4,3,2,1,0:T(2,128)(2,1)S(1)}, bf16[1,2,2,128,2,256]{5,4,3,2,1,0:T(2,128)(2,1)S(1)}, bf16[1,2,2,128,2,256]{5,4,3,2,1,0:T(2,...) fusion(bf16[8,2,2,128,2,256]{5,4,3,2,1,0:T(2,128)(2,1)} %param.5), kind=kLoop, calls=%fused_computation.119 | loop fusion | bytes 8388608 | tf_op jit(solution)/shard_map/slice | solution.py:26
  11.9 2.0 copy.180
  14.0 0.0 all-gather.17.cloned.1.call-update
  14.0 0.0 all-gather.19.cloned.1.call-start
  14.0 1.9 copy.183
  16.0 0.0 all-gather.19.cloned.1.call-update
  16.0 0.0 all-gather.21.cloned.1.call-start
  16.0 0.9 copy.186
  16.9 0.0 all-gather.21.cloned.1.call-update
  16.9 0.0 all-gather.23.cloned.1.call-start
  17.0 0.9 copy.189
  17.8 0.0 all-gather.23.cloned.1.call-update
  17.9 0.0 all-gather.25.cloned.1.call-start
  17.9 0.9 copy.192
  18.8 0.0 all-gather.25.cloned.1.call-update
  18.8 0.0 all-gather.27.cloned.1.call-start
  18.9 0.9 copy.195
  19.8 0.0 all-gather.27.cloned.1.call-update
  19.8 7.3 %all-to-all-start = ((bf16[1,32,2,2,256,32]{4,5,3,2,0,1:T(8,128)(2,1)}), bf16[1,32,2,2,256,32]{4,5,3,2,0,1:T(8,128)(2,1)S(1)}, u32[]{:S(2)}, u32[]{:S(2)}) async-start(bf16[1,32,2,2,256,32]{4,5,3,2,0,1:T(8,128)(2,1)} %bitcast.455), calls=%async_computation | async-start | bytes 4194304 | tf_op jit(solution)/shard_map/all_to_all | solution.py:36
  27.1 0.0 copy-start.1
  27.1 0.0 copy-start
  27.1 0.0 all-gather.29.cloned.1.call-start
  27.2 0.9 copy.198
  28.1 0.0 all-gather.29.cloned.1.call-update
  28.1 0.2 all-gather.31.cloned.1.call-start
  28.3 0.9 copy.201
  29.2 0.0 all-gather.31.cloned.1.call-update
  29.2 0.0 copy-done.1
  29.2 0.7 fusion.40
  34.8 0.0 copy-done
  34.8 0.2 select_reduce_fusion.1
  34.9 0.2 select_reduce_fusion
  35.2 40.1 %all-to-all-done = bf16[1,32,2,2,256,32]{4,5,3,2,0,1:T(8,128)(2,1)S(1)} async-done(((bf16[1,32,2,2,256,32]{4,5,3,2,0,1:T(8,128)(2,1)}), bf16[1,32,2,2,256,32]{4,5,3,2,0,1:T(8,128)(2,1)S(1)}, u32[]{:S(2)}, u32[]{:S(2)}) %all-to-all-start) | async-done | bytes 2097184 | tf_op jit(solution)/shard_map/all_to_all | solution.py:36
  75.4 1.6 copy.107
  76.9 0.0 all-gather.17.cloned.1.call-done
  76.9 4.3 %convolution_bitcast_fusion.7 = f32[1,4,2,2,2,256,256]{5,6,2,1,4,3,0:T(8,128)S(1)} fusion(bf16[4,2,2,256,256,1,1]{3,4,2,1,0,6,5:T(8,128)(2,1)} %bitcast.456, bf16[1,2,2,256,2,256]{3,5,2,4,1,0:T(8,128)(2,1)} %all-gather.17.cloned.1.call-done), kind=kOutput, calls=%fused_computation.8 | convolution fusion | flops 2147483648 | bytes 11534336 | tf_op jit(solution)/shard_map/ncphuv,thugw->ncptgvw/dot_general | solution.py:8
  81.2 1.0 subtract_convert_fusion.6
  82.2 0.0 all-gather.19.cloned.1.call-done
  82.2 3.8 %convolution_bitcast_fusion.6 = f32[1,4,2,2,2,256,256]{6,5,4,3,2,1,0:T(8,128)S(1)} fusion(bf16[1,2,2,256,2,256]{5,3,2,4,1,0:T(8,128)(2,1)} %all-gather.19.cloned.1.call-done, bf16[4,1,2,256,256]{3,4,0,2,1:T(8,128)(2,1)S(1)} %get-tuple-element.28, bf16[4,1,2,256,256]{3,4,0,2,1:T(8,128)(2,1)S(1)} %get-tuple-element.27), kind=kOutput, calls=%fused_computation.7 | convolution fusion | flops 2148532224 | bytes 11534336 | tf_op jit(solution)/shard_map/ncphuv,thugw->ncptgvw/dot_general | solution.py:8
  86.1 1.0 subtract_convert_fusion.5
  87.1 0.0 all-gather.21.cloned.1.call-done
  87.1 3.6 %convolution_bitcast_fusion.5 = f32[1,4,2,2,2,256,256]{6,5,4,3,2,1,0:T(8,128)S(1)} fusion(bf16[1,2,2,256,2,256]{5,3,2,4,1,0:T(8,128)(2,1)} %all-gather.21.cloned.1.call-done, bf16[4,1,2,256,256]{4,3,2,0,1:T(8,128)(2,1)S(1)} %get-tuple-element.26, bf16[4,1,2,256,256]{4,3,2,0,1:T(8,128)(2,1)S(1)} %get-tuple-element.25), kind=kOutput, calls=%fused_computation.6 | convolution fusion | flops 2148532224 | bytes 11534336 | tf_op jit(solution)/shard_map/ncphuv,thugw->ncptgvw/dot_general | solution.py:8
  90.7 1.0 subtract_convert_fusion.4
  91.7 0.0 all-gather.23.cloned.1.call-done
  91.8 3.7 %convolution_bitcast_fusion.4 = f32[1,4,2,2,2,256,256]{6,5,4,3,2,1,0:T(8,128)S(1)} fusion(bf16[1,2,2,256,2,256]{5,3,2,4,1,0:T(8,128)(2,1)} %all-gather.23.cloned.1.call-done, bf16[4,1,2,256,256]{4,3,2,0,1:T(8,128)(2,1)S(1)} %get-tuple-element.24, bf16[4,1,2,256,256]{4,3,2,0,1:T(8,128)(2,1)S(1)} %get-tuple-element.23), kind=kOutput, calls=%fused_computation.5 | convolution fusion | flops 2148532224 | bytes 11534336 | tf_op jit(solution)/shard_map/ncphuv,thugw->ncptgvw/dot_general | solution.py:8
  95.5 1.2 subtract_convert_fusion.3
  96.7 0.0 all-gather.25.cloned.1.call-done
  96.7 3.6 %convolution_bitcast_fusion.3 = f32[1,4,2,2,2,256,256]{6,5,4,3,2,1,0:T(8,128)S(1)} fusion(bf16[1,2,2,256,2,256]{5,3,2,4,1,0:T(8,128)(2,1)} %all-gather.25.cloned.1.call-done, bf16[4,1,2,256,256]{4,3,2,0,1:T(8,128)(2,1)S(1)} %get-tuple-element.22, bf16[4,1,2,256,256]{4,3,2,0,1:T(8,128)(2,1)S(1)} %get-tuple-element.21), kind=kOutput, calls=%fused_computation.4 | convolution fusion | flops 2148532224 | bytes 11534336 | tf_op jit(solution)/shard_map/ncphuv,thugw->ncptgvw/dot_general | solution.py:8
  100.4 1.0 subtract_convert_fusion.2
  101.4 0.0 all-gather.27.cloned.1.call-done
  101.4 3.6 %convolution_bitcast_fusion.2 = f32[1,4,2,2,2,256,256]{6,5,4,3,2,1,0:T(8,128)S(1)} fusion(bf16[1,2,2,256,2,256]{5,3,2,4,1,0:T(8,128)(2,1)} %all-gather.27.cloned.1.call-done, bf16[4,1,2,256,256]{4,3,2,0,1:T(8,128)(2,1)S(1)} %get-tuple-element.20, bf16[4,1,2,256,256]{4,3,2,0,1:T(8,128)(2,1)S(1)} %get-tuple-element.19), kind=kOutput, calls=%fused_computation.3 | convolution fusion | flops 2148532224 | bytes 11534336 | tf_op jit(solution)/shard_map/ncphuv,thugw->ncptgvw/dot_general | solution.py:8
  105.0 1.0 subtract_convert_fusion.1
  106.1 0.0 all-gather.29.cloned.1.call-done
  106.1 3.7 %convolution_bitcast_fusion.1 = f32[1,4,2,2,2,256,256]{6,5,4,3,2,1,0:T(8,128)S(1)} fusion(bf16[1,2,2,256,2,256]{5,3,2,4,1,0:T(8,128)(2,1)} %all-gather.29.cloned.1.call-done, bf16[4,1,2,256,256]{4,3,2,0,1:T(8,128)(2,1)S(1)} %get-tuple-element.18, bf16[4,1,2,256,256]{4,3,2,0,1:T(8,128)(2,1)S(1)} %get-tuple-element.17), kind=kOutput, calls=%fused_computation.2 | convolution fusion | flops 2148532224 | bytes 11534336 | tf_op jit(solution)/shard_map/ncphuv,thugw->ncptgvw/dot_general | solution.py:8
  109.7 1.0 subtract_convert_fusion
  110.7 0.0 all-gather.31.cloned.1.call-done
  110.8 3.6 %convolution_bitcast_fusion = f32[1,4,2,2,2,256,256]{6,5,4,3,2,1,0:T(8,128)S(1)} fusion(bf16[1,2,2,256,2,256]{5,3,2,4,1,0:T(8,128)(2,1)} %all-gather.31.cloned.1.call-done, bf16[4,1,2,256,256]{4,3,2,0,1:T(8,128)(2,1)S(1)} %get-tuple-element.16, bf16[4,1,2,256,256]{4,3,2,0,1:T(8,128)(2,1)S(1)} %get-tuple-element.15), kind=kOutput, calls=%fused_computation.1 | convolution fusion | flops 2148532224 | bytes 11534336 | tf_op jit(solution)/shard_map/ncphuv,thugw->ncptgvw/dot_general | solution.py:8
  114.4 0.7 multiply_subtract_fusion
  115.1 0.6 pad_maximum_fusion
  115.8 3.2 %copy.139 = f32[1,4,2,2,256,256]{5,3,1,2,0,4:T(2,128)S(1)} copy(f32[1,4,2,2,256,256]{5,4,3,1,2,0:T(8,128)S(1)} %pad_maximum_fusion) | data formatting | bytes 8388608 | tf_op jit(solution)/shard_map/stack | solution.py:15
  119.0 96.8 %all_to_all.33 = f32[1,4,2,2,256,256]{5,3,1,2,0,4:T(2,128)S(1)} all-to-all(f32[1,4,2,2,256,256]{5,3,1,2,0,4:T(2,128)S(1)} %copy.139), channel_id=1, replica_groups=mesh['cuts'=2,'wide'=8,'batch'=2] {'wide'}, dimensions={4} | all-to-all | bytes 8388608 | tf_op jit(solution)/shard_map/all_to_all | solution.py:41
  215.8 4.4 %copy.140 = f32[1,8,4,2,2,32,256]{6,5,4,3,2,1,0:T(8,128)} copy(f32[1,8,4,2,2,32,256]{6,4,2,3,5,1,0:T(2,128)S(1)} %bitcast.453) | data formatting | bytes 8388608 | tf_op jit(solution)/shard_map/all_to_all | solution.py:41
  (8 shorter events, 0.0 us)
Async XLA Ops:
  6.5 70.4 %all-gather.17.cloned.1.call-start = ((), (), s32[]{:S(2)}) async-start(), calls=%async_computation.2 | async-start | bytes 1572864 | tf_op jit(solution)/shard_map/all_gather | solution.py:26
  14.0 68.2 %all-gather.19.cloned.1.call-start = ((), (), s32[]{:S(2)}) async-start(), calls=%async_computation.3 | async-start | bytes 1572864 | tf_op jit(solution)/shard_map/all_gather | solution.py:26
  16.0 71.1 %all-gather.21.cloned.1.call-start = ((), (), s32[]{:S(2)}) async-start(), calls=%async_computation.4 | async-start | bytes 1572864 | tf_op jit(solution)/shard_map/all_gather | solution.py:26
  16.9 74.8 %all-gather.23.cloned.1.call-start = ((), (), s32[]{:S(2)}) async-start(), calls=%async_computation.5 | async-start | bytes 1572864 | tf_op jit(solution)/shard_map/all_gather | solution.py:26
  17.9 78.8 %all-gather.25.cloned.1.call-start = ((), (), s32[]{:S(2)}) async-start(), calls=%async_computation.6 | async-start | bytes 1572864 | tf_op jit(solution)/shard_map/all_gather | solution.py:26
  18.8 82.6 %all-gather.27.cloned.1.call-start = ((), (), s32[]{:S(2)}) async-start(), calls=%async_computation.7 | async-start | bytes 1572864 | tf_op jit(solution)/shard_map/all_gather | solution.py:26
  19.8 55.6 %all-to-all-start = ((bf16[1,32,2,2,256,32]{4,5,3,2,0,1:T(8,128)(2,1)}), bf16[1,32,2,2,256,32]{4,5,3,2,0,1:T(8,128)(2,1)S(1)}, u32[]{:S(2)}, u32[]{:S(2)}) async-start(bf16[1,32,2,2,256,32]{4,5,3,2,0,1:T(8,128)(2,1)} %bitcast.455), calls=%async_computation | async-start | bytes 4194304 | tf_op jit(solution)/shard_map/all_to_all | solution.py:36
  27.1 2.1 copy-start.1
  27.1 7.6 %copy-start = (f32[8,2,2,2]{0,3,2,1:T(2,128)S(1)}, f32[8,2,2,2]{0,3,2,1:T(2,128)}, u32[]{:S(2)}) copy-start(f32[8,2,2,2]{0,3,2,1:T(2,128)} %param.6) | copy-start | bytes 772
  27.1 78.9 %all-gather.29.cloned.1.call-start = ((), (), s32[]{:S(2)}) async-start(), calls=%async_computation.8 | async-start | bytes 1572864 | tf_op jit(solution)/shard_map/all_gather | solution.py:26
  28.1 82.7 %all-gather.31.cloned.1.call-start = ((), (), s32[]{:S(2)}) async-start(), calls=%async_computation.9 | async-start | bytes 1572864 | tf_op jit(solution)/shard_map/all_gather | solution.py:26
Sparse Core Ops, SparseCore 0:
  14.1 11.4 all-gather.16
  27.2 10.2 all-gather.18
  39.0 10.1 all-gather.20
  50.6 10.1 all-gather.22
  62.3 10.1 all-gather.24
  73.9 10.1 all-gather.26
  85.7 10.1 all-gather.28
  97.5 10.1 all-gather.30
where the time goes:
time: 228 us; the launch traced here: 227 us
  blocking collectives  96.8 us (42%)
  waiting for transfers between devices  40.4 us (18%)
  matrix products  30 us (13%)
  local copies, waits for them, and re-layouts  24.5 us (11%)
  between operations  18.6 us (8%)
  other arithmetic  8.93 us (4%)
  starting transfers between devices  7.8 us (3%)
    all_to_all x1, blocking collectives, shards(): lax.all_to_all(state, 'wide', split_axis=4, concat_axis=1, tiled=True)  96.8 us
    all_to_all x1, waiting for transfers between devices, shards(): lax.all_to_all(initial, 'wide', split_axis=1, concat_axis=5, tiled=True)  40.1 us
    dot_general x8, matrix products, contract(): jnp.einsum('ncphuv,thugw->ncptgvw', state, branch, preferred_element_type...  30 us
    unnamed x12, local copies, waits for them, and re-layouts  9.2 us
    all_to_all x1, starting transfers between devices, shards(): lax.all_to_all(initial, 'wide', split_axis=1, concat_axis=5, tiled=True)  7.32 us
    another operation x7, other arithmetic  7.23 us
    slice x1, local copies, waits for them, and re-layouts, branch_of(): return lax.all_gather(branches[step], 'batch', axis=2, tiled=True)  5.41 us
  transfers between devices with their start and end apart: 9, of which 1 were waited for; matrix products, arithmetic and copies ran while one was open for 19% of the time, Pallas kernels for 0%

commit v1 on v0

v1 whole, which is shorter than its diff:
```python
import functools

import jax
import jax.numpy as jnp
from jax import lax
from jax.experimental import pallas as pl
from jax.experimental.pallas import tpu as pltpu
from jax.sharding import PartitionSpec as P

MESH = pl.DeviceIdType.MESH
F32 = jnp.float32
BF16 = jnp.bfloat16


def dot(a, b, dims):
    return lax.dot_general(a, b, (dims, ((), ())), preferred_element_type=F32)


def kernel(wide, pair, x_ref, g_ref, proj_ref, bits_ref, out_ref,
           branch, recv1, send2, recv2, state,
           g_send, g_recv, g_local, s1_sem, r1_sem, l1_sem, s2_sem, r2_sem, l2_sem):
    me = lax.axis_index("wide")
    core = lax.axis_index("batch")
    steps = branch.shape[0]
    cols = recv1.shape[0]
    half = g_ref.shape[3]
    group = branch.shape[3]
    vch, width = recv1.shape[4], recv1.shape[5]
    order = sorted(range(1, wide), key=lambda k: (abs(2 * k - wide), k))

    barrier = pltpu.get_barrier_semaphore()
    for k in range(1, wide):
        pl.semaphore_signal(barrier, inc=1, device_id={"wide": lax.rem(me + k, wide)}, device_id_type=MESH)
    for k in range(1, pair):
        pl.semaphore_signal(barrier, inc=1, device_id={"batch": lax.rem(core + k, pair)}, device_id_type=MESH)
    pl.semaphore_wait(barrier, wide + pair - 2)

    def first(j, k):
        peer = lax.rem(me + k, wide)
        return pltpu.make_async_remote_copy(
            x_ref.at[peer, j], recv1.at[j, me], s1_sem.at[j, k], r1_sem.at[j, k],
            device_id={"wide": peer}, device_id_type=MESH)

    def first_own(j):
        return pltpu.make_async_copy(x_ref.at[me, j], recv1.at[j, me], l1_sem.at[j])

    def second(j, k):
        peer = lax.rem(me + k, wide)
        return pltpu.make_async_remote_copy(
            send2.at[j, peer], recv2.at[j, me], s2_sem.at[j, k], r2_sem.at[j, k],
            device_id={"wide": peer}, device_id_type=MESH)

    def second_own(j):
        return pltpu.make_async_copy(send2.at[j, me], recv2.at[j, me], l2_sem.at[j])

    def mine(s):
        return branch.at[s, :, :, pl.ds(pl.multiple_of(core * half, half), half), :]

    def share(s, k):
        return pltpu.make_async_remote_copy(
            g_ref.at[s], mine(s), g_send.at[s, k], g_recv.at[s, k],
            device_id={"batch": lax.rem(core + k, pair)}, device_id_type=MESH)

    def keep(s):
        return pltpu.make_async_copy(g_ref.at[s], mine(s), g_local.at[s])

    def send_column(j, carry):
        for k in order:
            first(j, k).start()
        first_own(j).start()
        return carry

    send_column(0, 0)

    def send_branch(s, carry):
        keep(s).start()
        for k in range(1, pair):
            share(s, k).start()
        return carry

    lax.fori_loop(0, steps, send_branch, 0)
    lax.fori_loop(1, cols, send_column, 0)

    def select(s, g):
        hit = bits_ref[0, s] == 1
        return (jnp.where(hit, proj_ref[s, 4 + g], proj_ref[s, g]),
                jnp.where(hit, proj_ref[s, 6 + g], proj_ref[s, 2 + g]))

    def apply(s, lhs, form, put):
        for g in range(2):
            lanes = pl.ds(g * width, width)
            weight = [branch[s, p, :, :, lanes].reshape(2 * group, width) for p in range(2)]
            if form == "flip":
                prod = [[dot(weight[t], lhs[p], ((0,), (0,))) for t in range(2)] for p in range(2)]
            else:
                axis = 1 if form == "rows" else 0
                prod = [[dot(lhs[p], weight[t], ((axis,), (0,))) for t in range(2)] for p in range(2)]
            re = prod[0][0] - prod[1][1]
            im = prod[0][1] + prod[1][0]
            sr, si = select(s, g)
            put(0, g, sr * re - si * im)
            put(1, g, sr * im + si * re)

    def gathered(buf, j):
        return [jnp.concatenate([buf[j, :, p, h].reshape(wide * vch, width) for h in range(2)], axis=1)
                for p in range(2)]

    def held(slot):
        return [state[slot, p].reshape(2 * group, width) for p in range(2)]

    def column(j, carry):
        for k in order:
            first(j, k).wait_recv()
        first_own(j).wait()

        @pl.when(j == 0)
        def _():
            def arrive(s, carry):
                keep(s).wait()
                for k in range(1, pair):
                    share(s, k).wait_recv()
                return carry
            lax.fori_loop(0, steps, arrive, 0)

        def put_state(slot):
            def put(p, g, value):
                state[slot, p, g] = value.astype(BF16)
            return put

        apply(0, gathered(recv1, j), "rows", put_state(0))

        def middle(s, carry):
            apply(s, held((s + 1) % 2), "columns", put_state(s % 2))
            return carry

        lax.fori_loop(1, steps - 2, middle, 0)

        def put_send(p, g, value):
            send2[j, :, p, g] = value.astype(BF16).reshape(wide, vch, width)

        apply(steps - 2, held((steps - 3) % 2), "flip", put_send)
        for k in order:
            second(j, k).start()
        second_own(j).start()
        return carry

    lax.fori_loop(0, cols, column, 0)

    def last(j, carry):
        for k in order:
            second(j, k).wait_recv()
        second_own(j).wait()

        def put_out(p, g, value):
            out_ref[:, j, p, g] = value.reshape(wide, vch, width)

        apply(steps - 1, gathered(recv2, j), "rows", put_out)
        return carry

    lax.fori_loop(0, cols, last, 0)

    def drain(j, carry):
        for k in order:
            first(j, k).wait_send()
            second(j, k).wait_send()
        return carry

    lax.fori_loop(0, cols, drain, 0)

    def drain_branch(s, carry):
        for k in range(1, pair):
            share(s, k).wait_send()
        return carry

    lax.fori_loop(0, steps, drain_branch, 0)


def solution(mesh):
    wide, pair = mesh.shape["wide"], mesh.shape["batch"]

    def shards(initial, branches, projectors, bits):
        _, columns, parts, shared, group, vch = initial.shape
        steps, half, width = branches.shape[0], branches.shape[3], branches.shape[5]
        cols = columns // wide
        x = jnp.swapaxes(initial, 4, 5).reshape(wide, cols, parts, shared, vch, group)
        g = branches.reshape(steps, parts, shared, half, shared * width)
        proj = projectors.reshape(steps, -1)
        dma = pltpu.SemaphoreType.DMA
        chunk = (cols, wide, parts, shared, vch, width)
        out = pl.pallas_call(
            functools.partial(kernel, wide, pair),
            out_shape=jax.ShapeDtypeStruct((wide, cols, parts, shared, vch, width), F32),
            in_specs=[
                pl.BlockSpec(memory_space=pl.ANY),
                pl.BlockSpec(memory_space=pl.ANY),
                pl.BlockSpec(memory_space=pltpu.SMEM),
                pl.BlockSpec(memory_space=pltpu.SMEM),
            ],
            out_specs=pl.BlockSpec(memory_space=pltpu.VMEM),
            scratch_shapes=[
                pltpu.VMEM((steps, parts, shared, half * pair, shared * width), BF16),
                pltpu.VMEM(chunk, BF16),
                pltpu.VMEM(chunk, BF16),
                pltpu.VMEM(chunk, BF16),
                pltpu.VMEM((2, parts, shared, group, width), BF16),
                dma((steps, pair)), dma((steps, pair)), dma((steps,)),
                dma((cols, wide)), dma((cols, wide)), dma((cols,)),
                dma((cols, wide)), dma((cols, wide)), dma((cols,)),
            ],
            compiler_params=pltpu.CompilerParams(
                collective_id=0, has_side_effects=True, vmem_limit_bytes=48 * 1024 * 1024),
        )(x, g, proj, bits)
        return out.reshape(1, columns, parts, shared, vch, width)

    in_specs = (
        P("batch", "cuts", None, None, None, "wide"),
        P(None, None, None, "batch", None, None),
        P(),
        P("batch", None),
    )
    out_specs = P("batch", "cuts", None, None, "wide", None)
    return jax.shard_map(shards, mesh=mesh, in_specs=in_specs, out_specs=out_specs, check_vma=False)
```

time: 228 us -> 113 us (0.50)
  Pallas kernels: 0 us -> 99.8 us
  blocking collectives: 96.8 us -> 0 us
  waiting for transfers between devices: 40.4 us -> 0 us
  matrix products: 30 us -> 0 us
  between operations: 18.6 us -> 0.01 us
  local copies, waits for them, and re-layouts: 24.5 us -> 13.3 us
  other arithmetic: 8.93 us -> 0 us
  starting transfers between devices: 7.8 us -> 0 us
    pallas_call x0 -> x1, Pallas kernels: none -> 99.8 us  [shards(): pl.pallas_call(functools.partial(kernel, wide, pair), out_shape=jax.Shape...]
    all_to_all x1 -> x0, blocking collectives: 96.8 us -> none  [shards(): lax.all_to_all(state, 'wide', split_axis=4, concat_axis=1, tiled=True)]
    all_to_all x1 -> x0, waiting for transfers between devices: 40.1 us -> none  [shards(): lax.all_to_all(initial, 'wide', split_axis=1, concat_axis=5, tiled=True)]
    dot_general x8 -> x0, matrix products: 30 us -> none  [contract(): jnp.einsum('ncphuv,thugw->ncptgvw', state, branch, preferred_element_type...]
    reshape x0 -> x2, local copies, waits for them, and re-layouts: none -> 8.49 us  [the longest x1 7.73 us: shards(): g = branches.reshape(steps, parts, shared, half, shared * width)]
    another operation x8 -> x0, other arithmetic: 7.87 us -> none
    all_to_all x1 -> x0, starting transfers between devices: 7.32 us -> none  [shards(): lax.all_to_all(initial, 'wide', split_axis=1, concat_axis=5, tiled=True)]
    slice x2 -> x0, local copies, waits for them, and re-layouts: 6.08 us -> none  [the longest x1 5.41 us: branch_of(): return lax.all_gather(branches[step], 'batch', axis=2, tiled=True)]
  transfers between devices with their start and end apart: 9 -> 0, of which waited for: 1 -> 0; matrix products, arithmetic and copies ran while one was open for 19% -> 0% of each run, Pallas kernels for 0% -> 0%
where the time goes in v1:
time: 113 us
  Pallas kernels  99.8 us (88%)
  local copies, waits for them, and re-layouts  13.3 us (12%)
    pallas_call x1, Pallas kernels, shards(): pl.pallas_call(functools.partial(kernel, wide, pair), out_shape=jax.Shape...  99.8 us
    reshape x1, local copies, waits for them, and re-layouts, shards(): g = branches.reshape(steps, parts, shared, half, shared * width)  7.73 us
    unnamed x5, local copies, waits for them, and re-layouts  4.8 us

profile of v1, /device:TPU:0, one launch (start us, length us, event | category | flops | bytes accessed | tf_op | source)
XLA Modules:
  0.0 113.0 jit_solution(16929782450331977245)
XLA Ops:
  0.0 0.8 copy.5.proj_ref
  0.8 0.0 copy-start
  0.8 0.0 copy-start.1
  0.8 7.7 %reshape.13.g_ref = bf16[8,2,2,128,512]{4,3,2,1,0:T(8,128)(2,1)} reshape(bf16[8,2,2,128,2,256]{5,4,3,2,1,0:T(2,128)(2,1)} %param.5) | data formatting | bytes 8388608 | tf_op jit(solution)/shard_map/reshape | solution.py:186
  8.5 0.0 copy-done
  8.5 0.0 copy-done.1
  8.5 99.8 %shard_map.46 = f32[8,4,2,2,32,256]{5,4,3,2,1,0:T(8,128)} custom-call(bf16[8,4,2,2,32,256]{5,4,3,2,1,0:T(8,128)(2,1)S(1)} %bitcast.5, bf16[8,2,2,128,512]{4,3,2,1,0:T(8,128)(2,1)} %reshape.13.g_ref, f32[8,8]{1,0:T(8,128)S(1)} %copy.5.proj_ref, s32[1,8]{1,0:T(1,128)S(1)} %copy-done.1), custom_call_target="tpu_custom_call" | custom-call | tf_op jit(solution)/shard_map/pallas_call | solution.py:190
  108.3 4.8 %copy.7 = f32[1,32,2,2,32,256]{5,4,3,2,1,0:T(8,128)} copy(f32[1,32,2,2,32,256]{5,4,3,2,1,0:T(8,128)} %bitcast.6) | data formatting | bytes 8388608
Async XLA Ops:
  0.8 7.7 %copy-start = (bf16[1,32,2,2,256,32]{4,5,3,2,1,0:T(8,128)(2,1)S(1)}, bf16[1,32,2,2,256,32]{4,5,3,2,1,0:T(8,128)(2,1)}, u32[]{:S(2)}) copy-start(bf16[1,32,2,2,256,32]{4,5,3,2,1,0:T(8,128)(2,1)} %param.4) | copy-start | bytes 6291460
  0.8 7.7 %copy-start.1 = (s32[1,8]{1,0:T(1,128)S(1)}, s32[1,8]{1,0:T(1,128)}, u32[]{:S(2)}) copy-start(s32[1,8]{1,0:T(1,128)} %bits_ref.1) | copy-start | bytes 100

commit v2 on v1

--- a/solution.py
+++ b/solution.py
@@ -17,14 +17,14 @@
 
 
 def kernel(wide, pair, x_ref, g_ref, proj_ref, bits_ref, out_ref,
-           branch, recv1, send2, recv2, state,
+           branch, recv1, send2, recv2, state, result, out_sem,
            g_send, g_recv, g_local, s1_sem, r1_sem, l1_sem, s2_sem, r2_sem, l2_sem):
     me = lax.axis_index("wide")
     core = lax.axis_index("batch")
     steps = branch.shape[0]
     cols = recv1.shape[0]
-    half = g_ref.shape[3]
-    group = branch.shape[3]
+    half = g_ref.shape[4]
+    group = branch.shape[4]
     vch, width = recv1.shape[4], recv1.shape[5]
     order = sorted(range(1, wide), key=lambda k: (abs(2 * k - wide), k))
 
@@ -54,7 +54,7 @@
         return pltpu.make_async_copy(send2.at[j, me], recv2.at[j, me], l2_sem.at[j])
 
     def mine(s):
-        return branch.at[s, :, :, pl.ds(pl.multiple_of(core * half, half), half), :]
+        return branch.at[s, :, :, :, pl.ds(pl.multiple_of(core * half, half), half), :]
 
     def share(s, k):
         return pltpu.make_async_remote_copy(
@@ -88,8 +88,7 @@
 
     def apply(s, lhs, form, put):
         for g in range(2):
-            lanes = pl.ds(g * width, width)
-            weight = [branch[s, p, :, :, lanes].reshape(2 * group, width) for p in range(2)]
+            weight = [branch[s, p, g].reshape(2 * group, width) for p in range(2)]
             if form == "flip":
                 prod = [[dot(weight[t], lhs[p], ((0,), (0,))) for t in range(2)] for p in range(2)]
             else:
@@ -146,15 +145,19 @@
 
     lax.fori_loop(0, cols, column, 0)
 
+    def leave(j):
+        return pltpu.make_async_copy(result.at[:, j], out_ref.at[:, j], out_sem.at[j])
+
     def last(j, carry):
         for k in order:
             second(j, k).wait_recv()
         second_own(j).wait()
 
         def put_out(p, g, value):
-            out_ref[:, j, p, g] = value.reshape(wide, vch, width)
+            result[:, j, p, g] = value.reshape(wide, vch, width)
 
         apply(steps - 1, gathered(recv2, j), "rows", put_out)
+        leave(j).start()
         return carry
 
     lax.fori_loop(0, cols, last, 0)
@@ -163,6 +166,7 @@
         for k in order:
             first(j, k).wait_send()
             second(j, k).wait_send()
+        leave(j).wait()
         return carry
 
     lax.fori_loop(0, cols, drain, 0)
@@ -183,32 +187,35 @@
         steps, half, width = branches.shape[0], branches.shape[3], branches.shape[5]
         cols = columns // wide
         x = jnp.swapaxes(initial, 4, 5).reshape(wide, cols, parts, shared, vch, group)
-        g = branches.reshape(steps, parts, shared, half, shared * width)
+        g = jnp.transpose(branches, (0, 1, 4, 2, 3, 5))
         proj = projectors.reshape(steps, -1)
         dma = pltpu.SemaphoreType.DMA
         chunk = (cols, wide, parts, shared, vch, width)
+        chunk_out = (wide, cols, parts, shared, vch, width)
         out = pl.pallas_call(
             functools.partial(kernel, wide, pair),
-            out_shape=jax.ShapeDtypeStruct((wide, cols, parts, shared, vch, width), F32),
+            out_shape=jax.ShapeDtypeStruct(chunk_out, F32),
             in_specs=[
                 pl.BlockSpec(memory_space=pl.ANY),
                 pl.BlockSpec(memory_space=pl.ANY),
                 pl.BlockSpec(memory_space=pltpu.SMEM),
                 pl.BlockSpec(memory_space=pltpu.SMEM),
             ],
-            out_specs=pl.BlockSpec(memory_space=pltpu.VMEM),
+            out_specs=pl.BlockSpec(memory_space=pl.ANY),
             scratch_shapes=[
-                pltpu.VMEM((steps, parts, shared, half * pair, shared * width), BF16),
+                pltpu.VMEM((steps, parts, shared, shared, half * pair, width), BF16),
                 pltpu.VMEM(chunk, BF16),
                 pltpu.VMEM(chunk, BF16),
                 pltpu.VMEM(chunk, BF16),
                 pltpu.VMEM((2, parts, shared, group, width), BF16),
+                pltpu.VMEM(chunk_out, F32),
+                dma((cols,)),
                 dma((steps, pair)), dma((steps, pair)), dma((steps,)),
                 dma((cols, wide)), dma((cols, wide)), dma((cols,)),
                 dma((cols, wide)), dma((cols, wide)), dma((cols,)),
             ],
             compiler_params=pltpu.CompilerParams(
-                collective_id=0, has_side_effects=True, vmem_limit_bytes=48 * 1024 * 1024),
+                collective_id=0, has_side_effects=True, vmem_limit_bytes=32 * 1024 * 1024),
         )(x, g, proj, bits)
         return out.reshape(1, columns, parts, shared, vch, width)
 

time: 113 us -> 104 us (0.920)
  local copies, waits for them, and re-layouts: 13.3 us -> 5.9 us
  Pallas kernels: 99.8 us -> 98 us
    reshape x1 -> x0, local copies, waits for them, and re-layouts: 7.73 us -> none  [shards(): g = branches.reshape(steps, parts, shared, half, shared * width)]
    pallas_call x1, Pallas kernels: 99.8 us -> 98 us  [shards(): pl.pallas_call(functools.partial(kernel, wide, pair), out_shape=jax.Shape...]
    unnamed x5 -> x6, local copies, waits for them, and re-layouts: 4.8 us -> 5.15 us
where the time goes in v2:
time: 104 us
  Pallas kernels  98 us (94%)
  local copies, waits for them, and re-layouts  5.9 us (6%)
    pallas_call x1, Pallas kernels, shards(): pl.pallas_call(functools.partial(kernel, wide, pair), out_shape=jax.Shape...  98 us
    unnamed x6, local copies, waits for them, and re-layouts  5.15 us

profile of v2, /device:TPU:0, one launch (start us, length us, event | category | flops | bytes accessed | tf_op | source)
XLA Modules:
  0.0 103.9 jit_solution(10233736800679633605)
XLA Ops:
  0.0 0.8 copy.6.proj_ref
  0.8 0.0 copy-start
  0.8 0.0 copy-start.1
  0.8 3.1 %copy.8 = bf16[8,2,2,128,2,256]{5,3,2,4,1,0:T(8,128)(2,1)S(1)} copy(bf16[8,2,2,128,2,256]{5,4,3,2,1,0:T(2,128)(2,1)} %param.5) | data formatting | bytes 8388608 | tf_op args[1]
  3.9 0.0 copy-done
  3.9 0.0 copy-done.1
  3.9 98.0 %shard_map.46 = f32[8,4,2,2,32,256]{5,4,3,2,1,0:T(8,128)S(1)} custom-call(bf16[8,4,2,2,32,256]{5,4,3,2,1,0:T(8,128)(2,1)S(1)} %bitcast.10, bf16[8,2,2,2,128,256]{5,4,3,2,1,0:T(8,128)(2,1)S(1)} %bitcast.9, f32[8,8]{1,0:T(8,128)S(1)} %copy.6.proj_ref, s32[1,8]{1,0:T(1,128)S(1)} %copy-done.1), custom_call_target="tpu_custom_call" | custom-call | tf_op jit(solution)/shard_map/pallas_call | solution.py:195
  101.9 2.0 %copy.10 = f32[1,32,2,2,32,256]{5,4,3,2,1,0:T(8,128)} copy(f32[1,32,2,2,32,256]{5,4,3,2,1,0:T(8,128)S(1)} %bitcast.8) | data formatting | bytes 8388608
Async XLA Ops:
  0.8 3.1 %copy-start = (bf16[1,32,2,2,256,32]{4,5,3,2,1,0:T(8,128)(2,1)S(1)}, bf16[1,32,2,2,256,32]{4,5,3,2,1,0:T(8,128)(2,1)}, u32[]{:S(2)}) copy-start(bf16[1,32,2,2,256,32]{4,5,3,2,1,0:T(8,128)(2,1)} %param.4) | copy-start | bytes 6291460
  0.8 3.1 %copy-start.1 = (s32[1,8]{1,0:T(1,128)S(1)}, s32[1,8]{1,0:T(1,128)}, u32[]{:S(2)}) copy-start(s32[1,8]{1,0:T(1,128)} %bits_ref.1) | copy-start | bytes 100

commit v3 on v2

--- a/solution.py
+++ b/solution.py
@@ -17,26 +17,35 @@
 
 
 def kernel(wide, pair, x_ref, g_ref, proj_ref, bits_ref, out_ref,
-           branch, recv1, send2, recv2, state, result, out_sem,
+           raw, branch, recv1, send2, recv2, state, result, out_sem,
            g_send, g_recv, g_local, s1_sem, r1_sem, l1_sem, s2_sem, r2_sem, l2_sem):
     me = lax.axis_index("wide")
     core = lax.axis_index("batch")
     steps = branch.shape[0]
     cols = recv1.shape[0]
-    half = g_ref.shape[4]
+    half = g_ref.shape[3]
     group = branch.shape[4]
     vch, width = recv1.shape[4], recv1.shape[5]
-    order = sorted(range(1, wide), key=lambda k: (abs(2 * k - wide), k))
+    near = range(1, wide)
+    far = sorted(near, key=lambda k: -k.bit_length())
+
+    def partner(k):
+        peer, bit = 0, 1
+        while bit < wide:
+            digit = lax.rem(me // bit, 2)
+            peer = peer + bit * (1 - digit if (k // bit) % 2 else digit)
+            bit *= 2
+        return peer
 
     barrier = pltpu.get_barrier_semaphore()
     for k in range(1, wide):
-        pl.semaphore_signal(barrier, inc=1, device_id={"wide": lax.rem(me + k, wide)}, device_id_type=MESH)
+        pl.semaphore_signal(barrier, inc=1, device_id={"wide": partner(k)}, device_id_type=MESH)
     for k in range(1, pair):
         pl.semaphore_signal(barrier, inc=1, device_id={"batch": lax.rem(core + k, pair)}, device_id_type=MESH)
     pl.semaphore_wait(barrier, wide + pair - 2)
 
     def first(j, k):
-        peer = lax.rem(me + k, wide)
+        peer = partner(k)
         return pltpu.make_async_remote_copy(
             x_ref.at[peer, j], recv1.at[j, me], s1_sem.at[j, k], r1_sem.at[j, k],
             device_id={"wide": peer}, device_id_type=MESH)
@@ -45,7 +54,7 @@
         return pltpu.make_async_copy(x_ref.at[me, j], recv1.at[j, me], l1_sem.at[j])
 
     def second(j, k):
-        peer = lax.rem(me + k, wide)
+        peer = partner(k)
         return pltpu.make_async_remote_copy(
             send2.at[j, peer], recv2.at[j, me], s2_sem.at[j, k], r2_sem.at[j, k],
             device_id={"wide": peer}, device_id_type=MESH)
@@ -54,7 +63,7 @@
         return pltpu.make_async_copy(send2.at[j, me], recv2.at[j, me], l2_sem.at[j])
 
     def mine(s):
-        return branch.at[s, :, :, :, pl.ds(pl.multiple_of(core * half, half), half), :]
+        return raw.at[s, :, :, pl.ds(pl.multiple_of(core * half, half), half)]
 
     def share(s, k):
         return pltpu.make_async_remote_copy(
@@ -65,12 +74,14 @@
         return pltpu.make_async_copy(g_ref.at[s], mine(s), g_local.at[s])
 
     def send_column(j, carry):
-        for k in order:
+        first_own(j).start()
+        for k in near:
             first(j, k).start()
-        first_own(j).start()
-        return carry
-
-    send_column(0, 0)
+        return carry
+
+    for k in far:
+        first(0, k).start()
+    first_own(0).start()
 
     def send_branch(s, carry):
         keep(s).start()
@@ -81,10 +92,22 @@
     lax.fori_loop(0, steps, send_branch, 0)
     lax.fori_loop(1, cols, send_column, 0)
 
+    def arrive(s, carry):
+        keep(s).wait()
+        for k in range(1, pair):
+            share(s, k).wait_recv()
+        for p in range(2):
+            for h in range(2):
+                both = raw[s, p, h]
+                for g in range(2):
+                    branch[s, p, g, h] = both[:, g, :]
+        return carry
+    lax.fori_loop(0, steps, arrive, 0)
+
     def select(s, g):
         hit = bits_ref[0, s] == 1
-        return (jnp.where(hit, proj_ref[s, 4 + g], proj_ref[s, g]),
-                jnp.where(hit, proj_ref[s, 6 + g], proj_ref[s, 2 + g]))
+        return (jnp.where(hit, proj_ref[4 + g, s], proj_ref[g, s]),
+                jnp.where(hit, proj_ref[6 + g, s], proj_ref[2 + g, s]))
 
     def apply(s, lhs, form, put):
         for g in range(2):
@@ -108,18 +131,9 @@
         return [state[slot, p].reshape(2 * group, width) for p in range(2)]
 
     def column(j, carry):
-        for k in order:
+        for k in near:
             first(j, k).wait_recv()
         first_own(j).wait()
-
-        @pl.when(j == 0)
-        def _():
-            def arrive(s, carry):
-                keep(s).wait()
-                for k in range(1, pair):
-                    share(s, k).wait_recv()
-                return carry
-            lax.fori_loop(0, steps, arrive, 0)
 
         def put_state(slot):
             def put(p, g, value):
@@ -138,7 +152,7 @@
             send2[j, :, p, g] = value.astype(BF16).reshape(wide, vch, width)
 
         apply(steps - 2, held((steps - 3) % 2), "flip", put_send)
-        for k in order:
+        for k in near:
             second(j, k).start()
         second_own(j).start()
         return carry
@@ -149,7 +163,7 @@
         return pltpu.make_async_copy(result.at[:, j], out_ref.at[:, j], out_sem.at[j])
 
     def last(j, carry):
-        for k in order:
+        for k in near:
             second(j, k).wait_recv()
         second_own(j).wait()
 
@@ -163,7 +177,7 @@
     lax.fori_loop(0, cols, last, 0)
 
     def drain(j, carry):
-        for k in order:
+        for k in near:
             first(j, k).wait_send()
             second(j, k).wait_send()
         leave(j).wait()
@@ -187,8 +201,7 @@
         steps, half, width = branches.shape[0], branches.shape[3], branches.shape[5]
         cols = columns // wide
         x = jnp.swapaxes(initial, 4, 5).reshape(wide, cols, parts, shared, vch, group)
-        g = jnp.transpose(branches, (0, 1, 4, 2, 3, 5))
-        proj = projectors.reshape(steps, -1)
+        proj = jnp.transpose(projectors, (1, 2, 3, 0)).reshape(-1, steps)
         dma = pltpu.SemaphoreType.DMA
         chunk = (cols, wide, parts, shared, vch, width)
         chunk_out = (wide, cols, parts, shared, vch, width)
@@ -196,13 +209,14 @@
             functools.partial(kernel, wide, pair),
             out_shape=jax.ShapeDtypeStruct(chunk_out, F32),
             in_specs=[
-                pl.BlockSpec(memory_space=pl.ANY),
-                pl.BlockSpec(memory_space=pl.ANY),
+                pl.BlockSpec(memory_space=pltpu.HBM),
+                pl.BlockSpec(memory_space=pltpu.HBM),
                 pl.BlockSpec(memory_space=pltpu.SMEM),
                 pl.BlockSpec(memory_space=pltpu.SMEM),
             ],
             out_specs=pl.BlockSpec(memory_space=pl.ANY),
             scratch_shapes=[
+                pltpu.VMEM((steps, parts, shared, half * pair, shared, width), BF16),
                 pltpu.VMEM((steps, parts, shared, shared, half * pair, width), BF16),
                 pltpu.VMEM(chunk, BF16),
                 pltpu.VMEM(chunk, BF16),
@@ -216,7 +230,7 @@
             ],
             compiler_params=pltpu.CompilerParams(
                 collective_id=0, has_side_effects=True, vmem_limit_bytes=32 * 1024 * 1024),
-        )(x, g, proj, bits)
+        )(x, branches, proj, bits)
         return out.reshape(1, columns, parts, shared, vch, width)
 
     in_specs = (

time: 104 us -> 105 us (level)
  local copies, waits for them, and re-layouts: 5.9 us -> 7.13 us
    unnamed x6 -> x9, local copies, waits for them, and re-layouts: 5.15 us -> 7.13 us
where the time goes in v3:
time: 105 us
  Pallas kernels  97.9 us (93%)
  local copies, waits for them, and re-layouts  7.13 us (7%)
    pallas_call x1, Pallas kernels, shards(): pl.pallas_call(functools.partial(kernel, wide, pair), out_shape=jax.Shape...  97.9 us
    unnamed x9, local copies, waits for them, and re-layouts  7.13 us

profile of v3, /device:TPU:0, one launch (start us, length us, event | category | flops | bytes accessed | tf_op | source)
XLA Modules:
  0.0 105.1 jit_solution(3046620821862399374)
XLA Ops:
  0.0 0.0 copy-start
  0.0 2.2 %copy-done = bf16[8,2,2,128,2,256]{5,4,3,2,1,0:T(2,128)(2,1)S(1)} copy-done((bf16[8,2,2,128,2,256]{5,4,3,2,1,0:T(2,128)(2,1)S(1)}, bf16[8,2,2,128,2,256]{5,4,3,2,1,0:T(2,128)(2,1)}, u32[]{:S(2)}) %copy-start) | copy-done | bytes 4194328
  2.2 0.0 copy-start.1
  2.2 1.6 %copy-done.1 = bf16[1,32,2,2,256,32]{4,5,3,2,1,0:T(8,128)(2,1)S(1)} copy-done((bf16[1,32,2,2,256,32]{4,5,3,2,1,0:T(8,128)(2,1)S(1)}, bf16[1,32,2,2,256,32]{4,5,3,2,1,0:T(8,128)(2,1)}, u32[]{:S(2)}) %copy-start.1) | copy-done | bytes 2097176
  3.8 0.0 copy-start.2
  3.8 0.7 copy-done.2
  4.5 0.0 copy-start.3
  4.5 0.7 copy-done.3
  5.1 97.9 %shard_map.46 = f32[8,4,2,2,32,256]{5,4,3,2,1,0:T(8,128)S(1)} custom-call(bf16[8,4,2,2,32,256]{5,4,3,2,1,0:T(8,128)(2,1)S(1)} %bitcast.8, bf16[8,2,2,128,2,256]{5,4,3,2,1,0:T(2,128)(2,1)S(1)} %copy-done, f32[8,8]{1,0:T(8,128)S(1)} %bitcast.9, s32[1,8]{1,0:T(1,128)S(1)} %copy-done.3), custom_call_target="tpu_custom_call" | custom-call | tf_op jit(solution)/shard_map/pallas_call | solution.py:208
  103.1 2.0 %copy.6 = f32[1,32,2,2,32,256]{5,4,3,2,1,0:T(8,128)} copy(f32[1,32,2,2,32,256]{5,4,3,2,1,0:T(8,128)S(1)} %bitcast.7) | data formatting | bytes 8388608
Async XLA Ops:
  0.0 2.2 %copy-start = (bf16[8,2,2,128,2,256]{5,4,3,2,1,0:T(2,128)(2,1)S(1)}, bf16[8,2,2,128,2,256]{5,4,3,2,1,0:T(2,128)(2,1)}, u32[]{:S(2)}) copy-start(bf16[8,2,2,128,2,256]{5,4,3,2,1,0:T(2,128)(2,1)} %g_ref.1) | copy-start | bytes 12582916
  2.2 1.6 %copy-start.1 = (bf16[1,32,2,2,256,32]{4,5,3,2,1,0:T(8,128)(2,1)S(1)}, bf16[1,32,2,2,256,32]{4,5,3,2,1,0:T(8,128)(2,1)}, u32[]{:S(2)}) copy-start(bf16[1,32,2,2,256,32]{4,5,3,2,1,0:T(8,128)(2,1)} %param.4) | copy-start | bytes 6291460
  3.8 0.7 copy-start.2
  4.5 0.7 copy-start.3

commit v4 on v3

--- a/solution.py
+++ b/solution.py
@@ -229,7 +229,7 @@
                 dma((cols, wide)), dma((cols, wide)), dma((cols,)),
             ],
             compiler_params=pltpu.CompilerParams(
-                collective_id=0, has_side_effects=True, vmem_limit_bytes=32 * 1024 * 1024),
+                collective_id=0, has_side_effects=True, vmem_limit_bytes=44 * 1024 * 1024),
         )(x, branches, proj, bits)
         return out.reshape(1, columns, parts, shared, vch, width)
 

time: 105 us -> 103 us (0.981)
  local copies, waits for them, and re-layouts: 7.13 us -> 4.95 us
    unnamed x9 -> x7, local copies, waits for them, and re-layouts: 7.13 us -> 4.95 us
where the time goes in v4:
time: 103 us
  Pallas kernels  97.9 us (95%)
  local copies, waits for them, and re-layouts  4.95 us (5%)
    pallas_call x1, Pallas kernels, shards(): pl.pallas_call(functools.partial(kernel, wide, pair), out_shape=jax.Shape...  97.9 us
    unnamed x7, local copies, waits for them, and re-layouts  4.95 us

profile of v4, /device:TPU:0, one launch (start us, length us, event | category | flops | bytes accessed | tf_op | source)
XLA Modules:
  0.0 102.9 jit_solution(12853397090234441640)
XLA Ops:
  0.0 0.0 copy-start
  0.0 1.6 %copy-done = bf16[1,32,2,2,256,32]{4,5,3,2,1,0:T(8,128)(2,1)S(1)} copy-done((bf16[1,32,2,2,256,32]{4,5,3,2,1,0:T(8,128)(2,1)S(1)}, bf16[1,32,2,2,256,32]{4,5,3,2,1,0:T(8,128)(2,1)}, u32[]{:S(2)}) %copy-start) | copy-done | bytes 2097176
  1.6 0.0 copy-start.1
  1.6 0.7 copy-done.1
  2.3 0.0 copy-start.2
  2.3 0.7 copy-done.2
  2.9 97.9 %shard_map.46 = f32[8,4,2,2,32,256]{5,4,3,2,1,0:T(8,128)S(1)} custom-call(bf16[8,4,2,2,32,256]{5,4,3,2,1,0:T(8,128)(2,1)S(1)} %bitcast.8, bf16[8,2,2,128,2,256]{5,4,3,2,1,0:T(2,128)(2,1)} %g_ref.1, f32[8,8]{1,0:T(8,128)S(1)} %bitcast.9, s32[1,8]{1,0:T(1,128)S(1)} %copy-done.2), custom_call_target="tpu_custom_call" | custom-call | tf_op jit(solution)/shard_map/pallas_call | solution.py:208
  100.9 2.0 %copy.6 = f32[1,32,2,2,32,256]{5,4,3,2,1,0:T(8,128)} copy(f32[1,32,2,2,32,256]{5,4,3,2,1,0:T(8,128)S(1)} %bitcast.7) | data formatting | bytes 8388608
Async XLA Ops:
  0.0 1.6 %copy-start = (bf16[1,32,2,2,256,32]{4,5,3,2,1,0:T(8,128)(2,1)S(1)}, bf16[1,32,2,2,256,32]{4,5,3,2,1,0:T(8,128)(2,1)}, u32[]{:S(2)}) copy-start(bf16[1,32,2,2,256,32]{4,5,3,2,1,0:T(8,128)(2,1)} %param.4) | copy-start | bytes 6291460
  1.6 0.7 copy-start.1
  2.3 0.7 copy-start.2
